TPU v7x, 256 devices: a 4x2x16 block of a 4x16x16 slice. The times are simulated.
256 devices in a mesh: groups: 2 (over y), blk: 128 (over z, x, core).
Axes of the slice: x: 4, y: 2, z: 16, core: 2. Of those that a mesh axis runs over, the one named last changes fastest.
The devices are a block of a 4x16x16 slice.
Arguments:
- positions: float32 [3, 65536], P(None, ('groups', 'blk')), parts along dimension 1, may hold values from 0 to 96
- right_side: float32 [3, 65536], P(None, ('groups', 'blk')), parts along dimension 1, may hold values from -18 to 18
- neighbours: int32 [16, 65536], P(None, ('groups', 'blk')), parts along dimension 1, may hold values from 0 to 32767, as said below
- counts: int32 [65536], P(('groups', 'blk')), parts along dimension 0, may hold values from 1 to 16
Outputs:
- solution: float32 [3, 65536], P(None, ('groups', 'blk')), parts along dimension 1
- residual: float32 [3, 65536], P(None, ('groups', 'blk')), parts along dimension 1
There are 2 independent parts, one for each index of `groups`. A program takes and returns all parts, laid end to end along the dimension named above; each array names one. Nothing has to cross between parts.
Inputs may be any that keep to these rules, and one draw needn't show every extreme that they name: `neighbours`: every entry in column i lies within 32 of i, counted cyclically over the 32768 particles.
All inputs are finite; a program needn't handle non-finite values.
Results may differ from a plain program's by a relative error of at most 0.0003.
Values sent between devices are 32-bit elements; how exact they have to be, the bound alone decides.
A program may use at most 64 MiB of HBM per device.

v0:
```python
import functools
import math
import jax
import jax.numpy as jnp
from jax import lax
from jax.sharding import Mesh
from jax.sharding import PartitionSpec as P

REACH = 32
ITERS = 2
BLK = ("blk_0", "blk_1", "blk_2")
GROUPS_BLK = ("groups", "blk_0", "blk_1", "blk_2")
SOFT = 0.0001
EPS = 1e-06


def extended_2(cells, sides, width):
    for axis, dim in sides:
        count = lax.axis_size(axis)
        head = lax.slice_in_dim(cells, 0, width, axis=dim)
        tail = lax.slice_in_dim(cells, cells.shape[dim] - width, cells.shape[dim], axis=dim)
        cells = jnp.concatenate(
            [
                lax.ppermute(tail, axis, [(i, (i + 1) % count) for i in range(count)]),
                cells,
                lax.ppermute(head, axis, [((i + 1) % count, i) for i in range(count)]),
            ],
            axis=dim,
        )
    return cells


def joined_along(tiles, dim):
    lengths = list(tiles.shape[1:])
    lengths[dim] *= tiles.shape[0]
    return jnp.moveaxis(tiles, 0, dim).reshape(lengths)


def stacked_from(array, axes, turns):
    tiles = array[None]
    for k in turns:
        tiles = lax.all_gather(tiles, axes[k], axis=0, tiled=True)
    held = [lax.axis_size(axes[k]) for k in reversed(turns)]
    tiles = tiles.reshape(*held, *array.shape)
    turned = sorted(range(len(turns)), key=lambda place: turns[len(turns) - 1 - place])
    return tiles.transpose(*turned, *range(len(turns), tiles.ndim)).reshape(-1, *array.shape)


def gathered_by_axis(array, axes, turns, dim):
    return joined_along(stacked_from(array, axes, turns), dim)


def one_axis_at_a_time(array, axes):
    return functools.reduce(lax.psum, axes, array)


def pair_coefficients(dx, dy, dz):
    dist = jnp.sqrt(dx * dx + dy * dy + dz * dz + SOFT)
    inverse = 1.0 / dist
    cube = inverse * inverse * inverse
    correlation = dist < 2.0
    coef_a = jnp.where(correlation, 1.0 - 9.0 * dist / 32.0, 0.75 * inverse + 0.5 * cube)
    coef_b = jnp.where(
        correlation, 3.0 / 32.0 * inverse, 0.75 * cube - 1.5 * cube * inverse * inverse
    )
    return (coef_a, coef_b)


def far_tile(row_pos, col_pos, col_vec):
    dx = row_pos[0][:, None] - col_pos[0][None, :]
    dy = row_pos[1][:, None] - col_pos[1][None, :]
    dz = row_pos[2][:, None] - col_pos[2][None, :]
    coef_a, coef_b = pair_coefficients(dx, dy, dz)
    along = dx * col_vec[0][None, :] + dy * col_vec[1][None, :] + dz * col_vec[2][None, :]
    weighted = coef_b * along
    out_x = jnp.sum(coef_a * col_vec[0][None, :] + weighted * dx, axis=1)
    out_y = jnp.sum(coef_a * col_vec[1][None, :] + weighted * dy, axis=1)
    out_z = jnp.sum(coef_a * col_vec[2][None, :] + weighted * dz, axis=1)
    return jnp.stack([out_x, out_y, out_z])


def far_piece(row_pos, col_pos, col_vec):
    width = col_pos.shape[1]
    size = math.gcd(width, 4096)
    count = width // size
    stacked_pos = col_pos.reshape(3, count, size).transpose(1, 0, 2)
    stacked_vec = col_vec.reshape(3, count, size).transpose(1, 0, 2)

    def advance(carry, item):
        return (carry + far_tile(row_pos, item[0], item[1]), None)

    start_sum = jnp.zeros((3, row_pos.shape[1]), jnp.float32)
    result, unused = lax.scan(advance, start_sum, (stacked_pos, stacked_vec))
    return result


def lubrication(positions, vec, near_pos, near_vec, live):
    delta = positions[:, None, :] - near_pos
    square = jnp.sum(delta * delta, axis=0) + SOFT
    dist = jnp.sqrt(square)
    strength = live / ((0.5 + jnp.abs(dist - 2.0)) * square)
    along = jnp.sum(delta * (vec[:, None, :] - near_vec), axis=0)
    return jnp.sum(delta * (strength * along)[None], axis=1)


def on_device(positions, right_side, neighbours, counts):
    rows = positions.shape[1]
    blocks = lax.axis_size(BLK)
    total = rows * blocks
    first_row = lax.axis_index(BLK) * rows
    slots = jnp.arange(neighbours.shape[0], dtype=jnp.int32)
    live = (slots[:, None] < counts[None, :]).astype(jnp.float32)
    local_slot = jnp.remainder(neighbours - first_row + REACH, total)
    beta = jnp.sqrt(one_axis_at_a_time(jnp.sum(right_side * right_side), BLK) + EPS)
    basis = [right_side / beta]
    images = []
    cosines = []
    sines = []
    rotated = [beta]
    columns = []
    for step in range(ITERS):
        vec = basis[step]
        stacked = jnp.concatenate([positions, vec], axis=0)
        extended = extended_2(stacked, ((BLK, 1),), REACH)
        picked = jnp.take(extended, local_slot, axis=1)
        gathered = gathered_by_axis(stacked, BLK, (1, 0, 2), 1)
        far = far_piece(positions, gathered[:3], gathered[3:])
        work = far + lubrication(positions, vec, picked[:3], picked[3:], live)
        images.append(work)
        local_terms = tuple((jnp.sum(work * basis[j]) for j in range(step + 1))) + (
            jnp.sum(work * work),
        )
        totals = jax.tree.map(lambda part: one_axis_at_a_time(part, BLK), local_terms)
        column = list(totals[: step + 1])
        squares = totals[step + 1]
        for j in range(step + 1):
            work = work - column[j] * basis[j]
            squares = squares - column[j] * column[j]
        below = jnp.sqrt(squares + EPS)
        basis.append(work / below)
        column.append(below)
        for j in range(step):
            first, second = (column[j], column[j + 1])
            column[j] = cosines[j] * first + sines[j] * second
            column[j + 1] = -sines[j] * first + cosines[j] * second
        pivot = jnp.sqrt(column[step] * column[step] + below * below)
        cosines.append(column[step] / pivot)
        sines.append(below / pivot)
        column[step] = pivot
        rotated.append(-sines[step] * rotated[step])
        rotated[step] = cosines[step] * rotated[step]
        columns.append(column)
    coeffs = [None] * ITERS
    for step in reversed(range(ITERS)):
        accum = rotated[step]
        for j in range(step + 1, ITERS):
            accum = accum - columns[j][step] * coeffs[j]
        coeffs[step] = accum / columns[step][step]
    solution = jnp.zeros_like(right_side)
    residual = right_side
    for step in range(ITERS):
        solution = solution + coeffs[step] * basis[step]
        residual = residual - coeffs[step] * images[step]
    return (solution, residual)


def solution(mesh):
    torus = Mesh(
        mesh.devices.reshape(mesh.shape["groups"], 16, 4, 2), ("groups", "blk_0", "blk_1", "blk_2")
    )
    placed = (P(None, GROUPS_BLK), P(None, GROUPS_BLK), P(None, GROUPS_BLK), P(GROUPS_BLK))
    return jax.shard_map(
        on_device,
        mesh=torus,
        in_specs=placed,
        out_specs=(P(None, GROUPS_BLK), P(None, GROUPS_BLK)),
        check_vma=False,
    )
```

profile of v0, /device:TPU:33, one launch (start us, length us, event | category | flops | bytes accessed | tf_op | source)
XLA Modules:
  0.0 429.3 jit_solution(15191888906879357911)
XLA Ops:
  1.9 43.8 %psum.126 = f32[]{:T(128)} all-reduce(f32[]{:T(128)} %multiply_reduce_fusion.9), channel_id=1, replica_groups=mesh['groups'=2,'blk_0'=16,'blk_1'=4,'blk_2'=2] {'blk_0'}, use_global_device_ids=true, to_apply=%region_1.2 | all-reduce | flops 1 | bytes 8 | tf_op jit(solution)/shard_map/psum | solution.py:54
  45.7 9.5 %psum.127 = f32[]{:T(128)} all-reduce(f32[]{:T(128)} %psum.126), channel_id=1, replica_groups=mesh['groups'=2,'blk_0'=16,'blk_1'=4,'blk_2'=2] {'blk_1'}, use_global_device_ids=true, to_apply=%region_2.3 | all-reduce | flops 1 | bytes 8 | tf_op jit(solution)/shard_map/psum | solution.py:54
  55.2 12.4 %psum.128 = f32[]{:T(128)} all-reduce(f32[]{:T(128)} %psum.127), channel_id=1, replica_groups=mesh['groups'=2,'blk_0'=16,'blk_1'=4,'blk_2'=2] {'blk_2'}, use_global_device_ids=true, to_apply=%region_3.4 | all-reduce | flops 1 | bytes 8 | tf_op jit(solution)/shard_map/psum | solution.py:54
  71.8 9.1 %all-gather.2 = f32[4,6,256]{2,1,0:T(8,128)S(1)} all-gather(f32[1,6,256]{2,1,0:T(8,128)S(1)} %fusion.51), channel_id=2, replica_groups=mesh['groups'=2,'blk_0'=16,'blk_1'=4,'blk_2'=2] {'blk_1'}, dimensions={0}, use_global_device_ids=true | all-gather | bytes 30720 | tf_op jit(solution)/shard_map/all_gather | solution.py:42
  80.9 24.3 %all_gather.19 = f32[64,6,256]{2,1,0:T(8,128)S(1)} all-gather(f32[4,6,256]{2,1,0:T(8,128)S(1)} %all-gather.2), channel_id=1, replica_groups=mesh['groups'=2,'blk_0'=16,'blk_1'=4,'blk_2'=2] {'blk_0'}, dimensions={0}, use_global_device_ids=true | all-gather | bytes 417792 | tf_op jit(solution)/shard_map/all_gather | solution.py:42
  105.4 14.5 %all_gather.20 = f32[128,6,256]{2,0,1:T(8,128)S(1)} all-gather(f32[64,6,256]{2,0,1:T(8,128)S(1)} %copy.85), channel_id=1, replica_groups=mesh['groups'=2,'blk_0'=16,'blk_1'=4,'blk_2'=2] {'blk_2'}, dimensions={0}, use_global_device_ids=true | all-gather | bytes 1179648 | tf_op jit(solution)/shard_map/all_gather | solution.py:42
  122.1 66.1 %while.26 = (s32[]{:T(128)}, f32[3,256]{1,0:T(4,128)S(1)}, f32[3,256]{1,0:T(4,128)S(1)}, f32[8,3,4096]{2,1,0:T(4,128)S(1)}, f32[8,3,4096]{2,1,0:T(4,128)S(1)}, /*index=5*/s32[]{:T(128)}, s32[]{:T(128)}, s32[]{}, s32[]{}) while((s32[]{:T(128)}, f32[3,256]{1,0:T(4,128)S(1)}, f32[3,256]{1,0:T(4,128)S(1)}, ...), condition=%wide.region_8.9_spmd.clone, body=%wide.region_4.0_spmd.clone.sunk | while | flops 46139652 | bytes 316555 | solution.py:93
  122.2 8.1 %fusion.67 = (f32[256]{0:T(256)S(1)}, f32[256]{0:T(256)S(1)}, f32[256]{0:T(256)S(1)}) fusion(f32[4096]{0:T(1024)S(1)} %bitcast.120, f32[4096]{0:T(1024)S(1)} %bitcast.123, f32[256]{0:T(256)S(1)} %bitcast.140, f32[4096]{0:T(1024)S(1)} %bitcast.122, f32[256]{0:T(256)S(1)} %bitcast.139, f32[4096]{0:T(1024)S(1)} %bitcast.124, f32[256]{0:T(256)S(1)} %bitcast.138, ...), kind=kLoop, calls=%fused_computation.23.clone.1 | loop fusion | flops 46136576 | bytes 104448 | tf_op jit(solution)/shard_map/while/body/eval_jaxpr/reduce_sum | solution.py:76
  130.5 8.1 %fusion.67 = (f32[256]{0:T(256)S(1)}, f32[256]{0:T(256)S(1)}, f32[256]{0:T(256)S(1)}) fusion(f32[4096]{0:T(1024)S(1)} %bitcast.120, f32[4096]{0:T(1024)S(1)} %bitcast.123, f32[256]{0:T(256)S(1)} %bitcast.140, f32[4096]{0:T(1024)S(1)} %bitcast.122, f32[256]{0:T(256)S(1)} %bitcast.139, f32[4096]{0:T(1024)S(1)} %bitcast.124, f32[256]{0:T(256)S(1)} %bitcast.138, ...), kind=kLoop, calls=%fused_computation.23.clone.1 | loop fusion | flops 46136576 | bytes 104448 | tf_op jit(solution)/shard_map/while/body/eval_jaxpr/reduce_sum | solution.py:76
  147.0 8.1 %fusion.67 = (f32[256]{0:T(256)S(1)}, f32[256]{0:T(256)S(1)}, f32[256]{0:T(256)S(1)}) fusion(f32[4096]{0:T(1024)S(1)} %bitcast.120, f32[4096]{0:T(1024)S(1)} %bitcast.123, f32[256]{0:T(256)S(1)} %bitcast.140, f32[4096]{0:T(1024)S(1)} %bitcast.122, f32[256]{0:T(256)S(1)} %bitcast.139, f32[4096]{0:T(1024)S(1)} %bitcast.124, f32[256]{0:T(256)S(1)} %bitcast.138, ...), kind=kLoop, calls=%fused_computation.23.clone.1 | loop fusion | flops 46136576 | bytes 104448 | tf_op jit(solution)/shard_map/while/body/eval_jaxpr/reduce_sum | solution.py:76
  155.3 8.1 %fusion.67 = (f32[256]{0:T(256)S(1)}, f32[256]{0:T(256)S(1)}, f32[256]{0:T(256)S(1)}) fusion(f32[4096]{0:T(1024)S(1)} %bitcast.120, f32[4096]{0:T(1024)S(1)} %bitcast.123, f32[256]{0:T(256)S(1)} %bitcast.140, f32[4096]{0:T(1024)S(1)} %bitcast.122, f32[256]{0:T(256)S(1)} %bitcast.139, f32[4096]{0:T(1024)S(1)} %bitcast.124, f32[256]{0:T(256)S(1)} %bitcast.138, ...), kind=kLoop, calls=%fused_computation.23.clone.1 | loop fusion | flops 46136576 | bytes 104448 | tf_op jit(solution)/shard_map/while/body/eval_jaxpr/reduce_sum | solution.py:76
  171.8 8.1 %fusion.67 = (f32[256]{0:T(256)S(1)}, f32[256]{0:T(256)S(1)}, f32[256]{0:T(256)S(1)}) fusion(f32[4096]{0:T(1024)S(1)} %bitcast.120, f32[4096]{0:T(1024)S(1)} %bitcast.123, f32[256]{0:T(256)S(1)} %bitcast.140, f32[4096]{0:T(1024)S(1)} %bitcast.122, f32[256]{0:T(256)S(1)} %bitcast.139, f32[4096]{0:T(1024)S(1)} %bitcast.124, f32[256]{0:T(256)S(1)} %bitcast.138, ...), kind=kLoop, calls=%fused_computation.23.clone.1 | loop fusion | flops 46136576 | bytes 104448 | tf_op jit(solution)/shard_map/while/body/eval_jaxpr/reduce_sum | solution.py:76
  180.1 8.1 %fusion.67 = (f32[256]{0:T(256)S(1)}, f32[256]{0:T(256)S(1)}, f32[256]{0:T(256)S(1)}) fusion(f32[4096]{0:T(1024)S(1)} %bitcast.120, f32[4096]{0:T(1024)S(1)} %bitcast.123, f32[256]{0:T(256)S(1)} %bitcast.140, f32[4096]{0:T(1024)S(1)} %bitcast.122, f32[256]{0:T(256)S(1)} %bitcast.139, f32[4096]{0:T(1024)S(1)} %bitcast.124, f32[256]{0:T(256)S(1)} %bitcast.138, ...), kind=kLoop, calls=%fused_computation.23.clone.1 | loop fusion | flops 46136576 | bytes 104448 | tf_op jit(solution)/shard_map/while/body/eval_jaxpr/reduce_sum | solution.py:76
  188.8 10.8 %gather_fusion = f32[4096,6]{1,0:T(8,128)S(1)} fusion(f32[6,320]{0,1:T(8,128)S(1)} %copy.90, s32[4096]{0:T(1024)S(1)} %broadcast_clamp_fusion), kind=kCustom, calls=%fused_computation.clone | custom fusion | bytes 212992 | tf_op jit(solution)/shard_map/jit(_take)/gather | solution.py:125
  203.5 22.6 %all-reduce.1 = (f32[]{:T(128)}, f32[]{:T(128)}) all-reduce(f32[]{:T(128)} %get-tuple-element.193, f32[]{:T(128)} %get-tuple-element.192), channel_id=1, replica_groups=mesh['groups'=2,'blk_0'=16,'blk_1'=4,'blk_2'=2] {'blk_0'}, use_global_device_ids=true, to_apply=%region_17.19 | all-reduce | flops 2 | bytes 16 | tf_op jit(solution)/shard_map/psum | solution.py:54
  233.0 11.8 %all-reduce.5 = (f32[]{:T(128)}, f32[]{:T(128)}) all-reduce(f32[]{:T(128)} %get-tuple-element.222, f32[]{:T(128)} %get-tuple-element.223), channel_id=1, replica_groups=mesh['groups'=2,'blk_0'=16,'blk_1'=4,'blk_2'=2] {'blk_2'}, use_global_device_ids=true, to_apply=%region_19.21 | all-reduce | flops 2 | bytes 16 | tf_op jit(solution)/shard_map/psum | solution.py:54
  249.5 9.3 %all-gather.3 = f32[4,6,256]{2,1,0:T(8,128)S(1)} all-gather(f32[1,6,256]{2,1,0:T(8,128)S(1)} %fusion.52), channel_id=3, replica_groups=mesh['groups'=2,'blk_0'=16,'blk_1'=4,'blk_2'=2] {'blk_1'}, dimensions={0}, use_global_device_ids=true | all-gather | bytes 30720 | tf_op jit(solution)/shard_map/all_gather | solution.py:42
  258.7 23.0 %all_gather.22 = f32[64,6,256]{2,1,0:T(8,128)S(1)} all-gather(f32[4,6,256]{2,1,0:T(8,128)S(1)} %all-gather.3), channel_id=1, replica_groups=mesh['groups'=2,'blk_0'=16,'blk_1'=4,'blk_2'=2] {'blk_0'}, dimensions={0}, use_global_device_ids=true | all-gather | bytes 417792 | tf_op jit(solution)/shard_map/all_gather | solution.py:42
  281.9 14.6 %all_gather.23 = f32[128,6,256]{2,0,1:T(8,128)S(1)} all-gather(f32[64,6,256]{2,0,1:T(8,128)S(1)} %copy.93), channel_id=1, replica_groups=mesh['groups'=2,'blk_0'=16,'blk_1'=4,'blk_2'=2] {'blk_2'}, dimensions={0}, use_global_device_ids=true | all-gather | bytes 1179648 | tf_op jit(solution)/shard_map/all_gather | solution.py:42
  298.7 66.1 %while.27 = (s32[]{:T(128)}, f32[3,256]{1,0:T(4,128)S(1)}, f32[3,256]{1,0:T(4,128)S(1)}, f32[8,3,4096]{2,1,0:T(4,128)S(1)}, f32[8,3,4096]{2,1,0:T(4,128)S(1)}, /*index=5*/s32[]{:T(128)}, s32[]{:T(128)}, s32[]{}, s32[]{}) while((s32[]{:T(128)}, f32[3,256]{1,0:T(4,128)S(1)}, f32[3,256]{1,0:T(4,128)S(1)}, ...), condition=%wide.region_24.26_spmd.clone, body=%wide.region_20.25_spmd.clone.sunk | while | flops 46139652 | bytes 316555 | solution.py:93
  298.8 8.1 %fusion.69 = (f32[256]{0:T(256)S(1)}, f32[256]{0:T(256)S(1)}, f32[256]{0:T(256)S(1)}) fusion(f32[4096]{0:T(1024)S(1)} %bitcast.126, f32[4096]{0:T(1024)S(1)} %bitcast.129, f32[256]{0:T(256)S(1)} %bitcast.143, f32[4096]{0:T(1024)S(1)} %bitcast.128, f32[256]{0:T(256)S(1)} %bitcast.142, f32[4096]{0:T(1024)S(1)} %bitcast.130, f32[256]{0:T(256)S(1)} %bitcast.141, ...), kind=kLoop, calls=%fused_computation.61.clone.1 | loop fusion | flops 46136576 | bytes 104448 | tf_op jit(solution)/shard_map/while/body/eval_jaxpr/reduce_sum | solution.py:76
  365.9 10.8 %gather_fusion.1 = f32[4096,6]{1,0:T(8,128)S(1)} fusion(f32[6,320]{0,1:T(8,128)S(1)} %copy.97, s32[4096]{0:T(1024)S(1)} %broadcast_clamp_fusion), kind=kCustom, calls=%fused_computation.1.clone | custom fusion | bytes 212992 | tf_op jit(solution)/shard_map/jit(_take)/gather | solution.py:125
  380.6 22.3 %all-reduce = (f32[]{:T(128)}, f32[]{:T(128)}, f32[]{:T(128)}) all-reduce(f32[]{:T(128)} %get-tuple-element.191, f32[]{:T(128)} %get-tuple-element.190, f32[]{:T(128)} %get-tuple-element.189), channel_id=1, replica_groups=mesh['groups'=2,'blk_0'=16,'blk_1'=4,'blk_2'=2] {'blk_0'}, use_global_device_ids=true, to_apply=%region_29.31 | all-reduce | flops 3 | bytes 24 | tf_op jit(solution)/shard_map/psum | solution.py:54
  409.5 12.4 %all-reduce.4 = (f32[]{:T(128)}, f32[]{:T(128)}, f32[]{:T(128)}) all-reduce(f32[]{:T(128)} %get-tuple-element.219, f32[]{:T(128)} %get-tuple-element.220, f32[]{:T(128)} %get-tuple-element.221), channel_id=1, replica_groups=mesh['groups'=2,'blk_0'=16,'blk_1'=4,'blk_2'=2] {'blk_2'}, use_global_device_ids=true, to_apply=%region_31.33 | all-reduce | flops 3 | bytes 24 | tf_op jit(solution)/shard_map/psum | solution.py:54
  (126 shorter events, 110.3 us)
Async XLA Ops:
  69.8 118.7 %collective-permute-start = (f32[6,32]{1,0:T(8,128)S(1)}, f32[6,32]{1,0:T(8,128)S(1)}, u32[]{:S(2)}, u32[]{:S(2)}) collective-permute-start(f32[6,32]{1,0:T(8,128)S(1)} %get-tuple-element.261), channel_id=1, source_target_pairs={{0,1},{1,2},{2,3},{3,4},{4,5},{5,6},{6,7},{7,8},{8,9},{9,10},{10,1... | collective-permute-start | bytes 2312 | tf_op jit(solution)/shard_map/ppermute | solution.py:24
  69.9 118.6 %collective-permute-start.1 = (f32[6,32]{1,0:T(8,128)S(1)}, f32[6,32]{1,0:T(8,128)S(1)}, u32[]{:S(2)}, u32[]{:S(2)}) collective-permute-start(f32[6,32]{1,0:T(8,128)S(1)} %get-tuple-element.262), channel_id=1, source_target_pairs={{1,0},{2,1},{3,2},{4,3},{5,4},{6,5},{7,6},{8,7},{9,8},{10,9},{11,1... | collective-permute-start | bytes 2312 | tf_op jit(solution)/shard_map/ppermute | solution.py:26
  121.3 0.7 copy-start
  122.1 66.1 %copy-start.2 = (s32[16,256]{1,0:T(8,128)S(1)}, s32[16,256]{1,0:T(8,128)}, u32[]{:S(2)}) copy-start(s32[16,256]{1,0:T(8,128)} %param.12) | copy-start | bytes 49156
  200.3 1.8 copy-start.3
  202.0 0.8 copy-start.1
  247.6 118.1 %collective-permute-start.2 = (f32[6,32]{1,0:T(8,128)S(1)}, f32[6,32]{1,0:T(8,128)S(1)}, u32[]{:S(2)}, u32[]{:S(2)}) collective-permute-start(f32[6,32]{1,0:T(8,128)S(1)} %get-tuple-element.259), channel_id=1, source_target_pairs={{0,1},{1,2},{2,3},{3,4},{4,5},{5,6},{6,7},{7,8},{8,9},{9,10},{10,1... | collective-permute-start | bytes 2312 | tf_op jit(solution)/shard_map/ppermute | solution.py:24
  249.5 116.2 %collective-permute-start.3 = (f32[6,32]{1,0:T(8,128)S(1)}, f32[6,32]{1,0:T(8,128)S(1)}, u32[]{:S(2)}, u32[]{:S(2)}) collective-permute-start(f32[6,32]{1,0:T(8,128)S(1)} %get-tuple-element.260), channel_id=1, source_target_pairs={{1,0},{2,1},{3,2},{4,3},{5,4},{6,5},{7,6},{8,7},{9,8},{10,9},{11,1... | collective-permute-start | bytes 2312 | tf_op jit(solution)/shard_map/ppermute | solution.py:26
where the time goes:
time: 430 us; the launch traced here: 429 us
  blocking collectives  243 us (57%)
  other arithmetic  144 us (33%)
  local copies, waits for them, and re-layouts  28.6 us (7%)
  between operations  10.7 us (2%)
    psum x9, blocking collectives, one_axis_at_a_time(): return functools.reduce(lax.psum, axes, array)  148 us
    reduce_sum x16, other arithmetic, far_tile(): out_x = jnp.sum(coef_a * col_vec[0][None, :] + weighted * dx, axis=1)  130 us
    all_gather x6, blocking collectives, stacked_from(): tiles = lax.all_gather(tiles, axes[k], axis=0, tiled=True)  94.7 us
    gather x2, local copies, waits for them, and re-layouts, on_device(): picked = jnp.take(extended, local_slot, axis=1)  21.6 us
  transfers between devices with their start and end apart: 4, of which 0 were waited for; matrix products, arithmetic and copies ran while one was open for 32% of the time, Pallas kernels for 0%

commit v1 on v0

--- a/solution.py
+++ b/solution.py
@@ -5,6 +5,7 @@
 from jax import lax
 from jax.sharding import Mesh
 from jax.sharding import PartitionSpec as P
+from jax.lax import all_to_all, axis_size
 
 REACH = 32
 ITERS = 2
@@ -39,7 +40,9 @@
 def stacked_from(array, axes, turns):
     tiles = array[None]
     for k in turns:
-        tiles = lax.all_gather(tiles, axes[k], axis=0, tiled=True)
+        obj = axes[k]
+        tall = jnp.stack([tiles] * axis_size(obj))
+        tiles = jnp.concatenate(all_to_all(tall, obj, split_axis=0, concat_axis=0), axis=0)
     held = [lax.axis_size(axes[k]) for k in reversed(turns)]
     tiles = tiles.reshape(*held, *array.shape)
     turned = sorted(range(len(turns)), key=lambda place: turns[len(turns) - 1 - place])

time: 430 us -> 402 us (0.935)
  blocking collectives: 243 us -> 190 us
  starting transfers between devices: 2.42 us -> 18.4 us
  waiting for transfers between devices: 0.01 us -> 5.36 us
    all_gather x6 -> x0, blocking collectives: 94.7 us -> none  [stacked_from(): tiles = lax.all_gather(tiles, axes[k], axis=0, tiled=True)]
    all_to_all x0 -> x3, blocking collectives: none -> 32 us  [stacked_from(): all_to_all(tall, obj, split_axis=0, concat_axis=0)]
    all_to_all x0 -> x3, starting transfers between devices: none -> 15.6 us  [stacked_from(): all_to_all(tall, obj, split_axis=0, concat_axis=0)]
    psum x9, blocking collectives: 148 us -> 158 us  [one_axis_at_a_time(): return functools.reduce(lax.psum, axes, array)]
  transfers between devices with their start and end apart: 4 -> 7, of which waited for: 0 -> 2; matrix products, arithmetic and copies ran while one was open for 32% -> 8% of each run, Pallas kernels for 0% -> 0%
where the time goes in v1:
time: 402 us; the launch traced here: 401 us
  blocking collectives  190 us (47%)
  other arithmetic  145 us (36%)
  local copies, waits for them, and re-layouts  31.1 us (8%)
  starting transfers between devices  18.4 us (5%)
  between operations  10.7 us (3%)
  waiting for transfers between devices  5.36 us (1%)
    psum x9, blocking collectives, one_axis_at_a_time(): return functools.reduce(lax.psum, axes, array)  158 us
    reduce_sum x16, other arithmetic, far_tile(): out_x = jnp.sum(coef_a * col_vec[0][None, :] + weighted * dx, axis=1)  130 us
    all_to_all x3, blocking collectives, stacked_from(): all_to_all(tall, obj, split_axis=0, concat_axis=0)  32 us
    gather x2, local copies, waits for them, and re-layouts, on_device(): picked = jnp.take(extended, local_slot, axis=1)  21.6 us
    all_to_all x3, starting transfers between devices, stacked_from(): all_to_all(tall, obj, split_axis=0, concat_axis=0)  15.6 us
  transfers between devices with their start and end apart: 7, of which 2 were waited for; matrix products, arithmetic and copies ran while one was open for 8% of the time, Pallas kernels for 0%

profile of v1, /device:TPU:33, one launch (start us, length us, event | category | flops | bytes accessed | tf_op | source)
XLA Modules:
  0.0 401.2 jit_solution(2598114479817961360)
XLA Ops:
  1.9 43.8 %psum.126 = f32[]{:T(128)} all-reduce(f32[]{:T(128)} %multiply_reduce_fusion.9), channel_id=1, replica_groups=mesh['groups'=2,'blk_0'=16,'blk_1'=4,'blk_2'=2] {'blk_0'}, use_global_device_ids=true, to_apply=%region_1.2 | all-reduce | flops 1 | bytes 8 | tf_op jit(solution)/shard_map/psum | solution.py:57
  45.7 9.5 %psum.127 = f32[]{:T(128)} all-reduce(f32[]{:T(128)} %psum.126), channel_id=1, replica_groups=mesh['groups'=2,'blk_0'=16,'blk_1'=4,'blk_2'=2] {'blk_1'}, use_global_device_ids=true, to_apply=%region_2.3 | all-reduce | flops 1 | bytes 8 | tf_op jit(solution)/shard_map/psum | solution.py:57
  55.2 12.4 %psum.128 = f32[]{:T(128)} all-reduce(f32[]{:T(128)} %psum.127), channel_id=1, replica_groups=mesh['groups'=2,'blk_0'=16,'blk_1'=4,'blk_2'=2] {'blk_2'}, use_global_device_ids=true, to_apply=%region_3.4 | all-reduce | flops 1 | bytes 8 | tf_op jit(solution)/shard_map/psum | solution.py:57
  87.7 10.8 %gather_fusion = f32[4096,6]{1,0:T(8,128)S(1)} fusion(f32[6,320]{0,1:T(8,128)S(1)} %copy.134, s32[4096]{0:T(1024)S(1)} %broadcast_clamp_fusion), kind=kCustom, calls=%fused_computation.clone | custom fusion | bytes 212992 | tf_op jit(solution)/shard_map/jit(_take)/gather | solution.py:128
  102.1 11.3 %all_to_all.30 = f32[2,64,6,256]{3,1,2,0:T(8,128)S(1)} all-to-all(f32[2,64,6,256]{3,1,2,0:T(8,128)S(1)} %pad_maximum_fusion), channel_id=1, replica_groups=mesh['groups'=2,'blk_0'=16,'blk_1'=4,'blk_2'=2] {'blk_2'}, dimensions={0} | all-to-all | bytes 1572864 | tf_op jit(solution)/shard_map/all_to_all | solution.py:45
  115.3 66.1 %while.26 = (s32[]{:T(128)}, f32[3,256]{1,0:T(4,128)S(1)}, f32[3,256]{1,0:T(4,128)S(1)}, f32[8,3,4096]{2,1,0:T(4,128)S(1)}, f32[8,3,4096]{2,1,0:T(4,128)S(1)}, /*index=5*/s32[]{:T(128)}, s32[]{:T(128)}, s32[]{}, s32[]{}) while((s32[]{:T(128)}, f32[3,256]{1,0:T(4,128)S(1)}, f32[3,256]{1,0:T(4,128)S(1)}, ...), condition=%wide.region_8.9_spmd.clone, body=%wide.region_4.0_spmd.clone.sunk | while | flops 46139652 | bytes 316555 | solution.py:96
  115.4 8.1 %fusion.65 = (f32[256]{0:T(256)S(1)}, f32[256]{0:T(256)S(1)}, f32[256]{0:T(256)S(1)}) fusion(f32[4096]{0:T(1024)S(1)} %bitcast.122, f32[4096]{0:T(1024)S(1)} %bitcast.125, f32[256]{0:T(256)S(1)} %bitcast.144, f32[4096]{0:T(1024)S(1)} %bitcast.124, f32[256]{0:T(256)S(1)} %bitcast.143, f32[4096]{0:T(1024)S(1)} %bitcast.126, f32[256]{0:T(256)S(1)} %bitcast.142, ...), kind=kLoop, calls=%fused_computation.23.clone.1 | loop fusion | flops 46136576 | bytes 104448 | tf_op jit(solution)/shard_map/while/body/eval_jaxpr/reduce_sum | solution.py:79
  132.0 8.1 %fusion.65 = (f32[256]{0:T(256)S(1)}, f32[256]{0:T(256)S(1)}, f32[256]{0:T(256)S(1)}) fusion(f32[4096]{0:T(1024)S(1)} %bitcast.122, f32[4096]{0:T(1024)S(1)} %bitcast.125, f32[256]{0:T(256)S(1)} %bitcast.144, f32[4096]{0:T(1024)S(1)} %bitcast.124, f32[256]{0:T(256)S(1)} %bitcast.143, f32[4096]{0:T(1024)S(1)} %bitcast.126, f32[256]{0:T(256)S(1)} %bitcast.142, ...), kind=kLoop, calls=%fused_computation.23.clone.1 | loop fusion | flops 46136576 | bytes 104448 | tf_op jit(solution)/shard_map/while/body/eval_jaxpr/reduce_sum | solution.py:79
  140.2 8.1 %fusion.65 = (f32[256]{0:T(256)S(1)}, f32[256]{0:T(256)S(1)}, f32[256]{0:T(256)S(1)}) fusion(f32[4096]{0:T(1024)S(1)} %bitcast.122, f32[4096]{0:T(1024)S(1)} %bitcast.125, f32[256]{0:T(256)S(1)} %bitcast.144, f32[4096]{0:T(1024)S(1)} %bitcast.124, f32[256]{0:T(256)S(1)} %bitcast.143, f32[4096]{0:T(1024)S(1)} %bitcast.126, f32[256]{0:T(256)S(1)} %bitcast.142, ...), kind=kLoop, calls=%fused_computation.23.clone.1 | loop fusion | flops 46136576 | bytes 104448 | tf_op jit(solution)/shard_map/while/body/eval_jaxpr/reduce_sum | solution.py:79
  148.5 8.1 %fusion.65 = (f32[256]{0:T(256)S(1)}, f32[256]{0:T(256)S(1)}, f32[256]{0:T(256)S(1)}) fusion(f32[4096]{0:T(1024)S(1)} %bitcast.122, f32[4096]{0:T(1024)S(1)} %bitcast.125, f32[256]{0:T(256)S(1)} %bitcast.144, f32[4096]{0:T(1024)S(1)} %bitcast.124, f32[256]{0:T(256)S(1)} %bitcast.143, f32[4096]{0:T(1024)S(1)} %bitcast.126, f32[256]{0:T(256)S(1)} %bitcast.142, ...), kind=kLoop, calls=%fused_computation.23.clone.1 | loop fusion | flops 46136576 | bytes 104448 | tf_op jit(solution)/shard_map/while/body/eval_jaxpr/reduce_sum | solution.py:79
  165.0 8.1 %fusion.65 = (f32[256]{0:T(256)S(1)}, f32[256]{0:T(256)S(1)}, f32[256]{0:T(256)S(1)}) fusion(f32[4096]{0:T(1024)S(1)} %bitcast.122, f32[4096]{0:T(1024)S(1)} %bitcast.125, f32[256]{0:T(256)S(1)} %bitcast.144, f32[4096]{0:T(1024)S(1)} %bitcast.124, f32[256]{0:T(256)S(1)} %bitcast.143, f32[4096]{0:T(1024)S(1)} %bitcast.126, f32[256]{0:T(256)S(1)} %bitcast.142, ...), kind=kLoop, calls=%fused_computation.23.clone.1 | loop fusion | flops 46136576 | bytes 104448 | tf_op jit(solution)/shard_map/while/body/eval_jaxpr/reduce_sum | solution.py:79
  173.3 8.1 %fusion.65 = (f32[256]{0:T(256)S(1)}, f32[256]{0:T(256)S(1)}, f32[256]{0:T(256)S(1)}) fusion(f32[4096]{0:T(1024)S(1)} %bitcast.122, f32[4096]{0:T(1024)S(1)} %bitcast.125, f32[256]{0:T(256)S(1)} %bitcast.144, f32[4096]{0:T(1024)S(1)} %bitcast.124, f32[256]{0:T(256)S(1)} %bitcast.143, f32[4096]{0:T(1024)S(1)} %bitcast.126, f32[256]{0:T(256)S(1)} %bitcast.142, ...), kind=kLoop, calls=%fused_computation.23.clone.1 | loop fusion | flops 46136576 | bytes 104448 | tf_op jit(solution)/shard_map/while/body/eval_jaxpr/reduce_sum | solution.py:79
  182.0 23.2 %all-reduce.1 = (f32[]{:T(128)}, f32[]{:T(128)}) all-reduce(f32[]{:T(128)} %get-tuple-element.195, f32[]{:T(128)} %get-tuple-element.194), channel_id=1, replica_groups=mesh['groups'=2,'blk_0'=16,'blk_1'=4,'blk_2'=2] {'blk_0'}, use_global_device_ids=true, to_apply=%region_17.19 | all-reduce | flops 2 | bytes 16 | tf_op jit(solution)/shard_map/psum | solution.py:57
  212.7 12.3 %all-reduce.5 = (f32[]{:T(128)}, f32[]{:T(128)}) all-reduce(f32[]{:T(128)} %get-tuple-element.224, f32[]{:T(128)} %get-tuple-element.225), channel_id=1, replica_groups=mesh['groups'=2,'blk_0'=16,'blk_1'=4,'blk_2'=2] {'blk_2'}, use_global_device_ids=true, to_apply=%region_19.21 | all-reduce | flops 2 | bytes 16 | tf_op jit(solution)/shard_map/psum | solution.py:57
  247.8 10.8 %gather_fusion.1 = f32[4096,6]{1,0:T(8,128)S(1)} fusion(f32[6,320]{0,1:T(8,128)S(1)} %copy.142, s32[4096]{0:T(1024)S(1)} %broadcast_clamp_fusion), kind=kCustom, calls=%fused_computation.1.clone | custom fusion | bytes 212992 | tf_op jit(solution)/shard_map/jit(_take)/gather | solution.py:128
  262.1 14.1 %all_to_all.32 = f32[2,64,6,256]{3,1,2,0:T(8,128)S(1)} all-to-all(f32[2,64,6,256]{3,1,2,0:T(8,128)S(1)} %pad_maximum_fusion.1), channel_id=1, replica_groups=mesh['groups'=2,'blk_0'=16,'blk_1'=4,'blk_2'=2] {'blk_2'}, dimensions={0} | all-to-all | bytes 1572864 | tf_op jit(solution)/shard_map/all_to_all | solution.py:45
  278.2 66.1 %while.27 = (s32[]{:T(128)}, f32[3,256]{1,0:T(4,128)S(1)}, f32[3,256]{1,0:T(4,128)S(1)}, f32[8,3,4096]{2,1,0:T(4,128)S(1)}, f32[8,3,4096]{2,1,0:T(4,128)S(1)}, /*index=5*/s32[]{:T(128)}, s32[]{:T(128)}, s32[]{}, s32[]{}) while((s32[]{:T(128)}, f32[3,256]{1,0:T(4,128)S(1)}, f32[3,256]{1,0:T(4,128)S(1)}, ...), condition=%wide.region_24.26_spmd.clone, body=%wide.region_20.25_spmd.clone.sunk | while | flops 46139652 | bytes 316555 | solution.py:96
  278.3 8.1 %fusion.67 = (f32[256]{0:T(256)S(1)}, f32[256]{0:T(256)S(1)}, f32[256]{0:T(256)S(1)}) fusion(f32[4096]{0:T(1024)S(1)} %bitcast.128, f32[4096]{0:T(1024)S(1)} %bitcast.131, f32[256]{0:T(256)S(1)} %bitcast.147, f32[4096]{0:T(1024)S(1)} %bitcast.130, f32[256]{0:T(256)S(1)} %bitcast.146, f32[4096]{0:T(1024)S(1)} %bitcast.132, f32[256]{0:T(256)S(1)} %bitcast.145, ...), kind=kLoop, calls=%fused_computation.61.clone.1 | loop fusion | flops 46136576 | bytes 104448 | tf_op jit(solution)/shard_map/while/body/eval_jaxpr/reduce_sum | solution.py:79
  286.6 8.1 %fusion.67 = (f32[256]{0:T(256)S(1)}, f32[256]{0:T(256)S(1)}, f32[256]{0:T(256)S(1)}) fusion(f32[4096]{0:T(1024)S(1)} %bitcast.128, f32[4096]{0:T(1024)S(1)} %bitcast.131, f32[256]{0:T(256)S(1)} %bitcast.147, f32[4096]{0:T(1024)S(1)} %bitcast.130, f32[256]{0:T(256)S(1)} %bitcast.146, f32[4096]{0:T(1024)S(1)} %bitcast.132, f32[256]{0:T(256)S(1)} %bitcast.145, ...), kind=kLoop, calls=%fused_computation.61.clone.1 | loop fusion | flops 46136576 | bytes 104448 | tf_op jit(solution)/shard_map/while/body/eval_jaxpr/reduce_sum | solution.py:79
  294.8 8.1 %fusion.67 = (f32[256]{0:T(256)S(1)}, f32[256]{0:T(256)S(1)}, f32[256]{0:T(256)S(1)}) fusion(f32[4096]{0:T(1024)S(1)} %bitcast.128, f32[4096]{0:T(1024)S(1)} %bitcast.131, f32[256]{0:T(256)S(1)} %bitcast.147, f32[4096]{0:T(1024)S(1)} %bitcast.130, f32[256]{0:T(256)S(1)} %bitcast.146, f32[4096]{0:T(1024)S(1)} %bitcast.132, f32[256]{0:T(256)S(1)} %bitcast.145, ...), kind=kLoop, calls=%fused_computation.61.clone.1 | loop fusion | flops 46136576 | bytes 104448 | tf_op jit(solution)/shard_map/while/body/eval_jaxpr/reduce_sum | solution.py:79
  311.4 8.1 %fusion.67 = (f32[256]{0:T(256)S(1)}, f32[256]{0:T(256)S(1)}, f32[256]{0:T(256)S(1)}) fusion(f32[4096]{0:T(1024)S(1)} %bitcast.128, f32[4096]{0:T(1024)S(1)} %bitcast.131, f32[256]{0:T(256)S(1)} %bitcast.147, f32[4096]{0:T(1024)S(1)} %bitcast.130, f32[256]{0:T(256)S(1)} %bitcast.146, f32[4096]{0:T(1024)S(1)} %bitcast.132, f32[256]{0:T(256)S(1)} %bitcast.145, ...), kind=kLoop, calls=%fused_computation.61.clone.1 | loop fusion | flops 46136576 | bytes 104448 | tf_op jit(solution)/shard_map/while/body/eval_jaxpr/reduce_sum | solution.py:79
  344.9 26.6 %all-reduce = (f32[]{:T(128)}, f32[]{:T(128)}, f32[]{:T(128)}) all-reduce(f32[]{:T(128)} %get-tuple-element.193, f32[]{:T(128)} %get-tuple-element.192, f32[]{:T(128)} %get-tuple-element.191), channel_id=1, replica_groups=mesh['groups'=2,'blk_0'=16,'blk_1'=4,'blk_2'=2] {'blk_0'}, use_global_device_ids=true, to_apply=%region_29.31 | all-reduce | flops 3 | bytes 24 | tf_op jit(solution)/shard_map/psum | solution.py:57
  371.4 10.3 %all-reduce.2 = (f32[]{:T(128)}, f32[]{:T(128)}, f32[]{:T(128)}) all-reduce(f32[]{:T(128)} %get-tuple-element.216, f32[]{:T(128)} %get-tuple-element.217, f32[]{:T(128)} %get-tuple-element.218), channel_id=1, replica_groups=mesh['groups'=2,'blk_0'=16,'blk_1'=4,'blk_2'=2] {'blk_1'}, use_global_device_ids=true, to_apply=%region_30.32 | all-reduce | flops 3 | bytes 24 | tf_op jit(solution)/shard_map/psum | solution.py:57
  381.8 12.1 %all-reduce.4 = (f32[]{:T(128)}, f32[]{:T(128)}, f32[]{:T(128)}) all-reduce(f32[]{:T(128)} %get-tuple-element.221, f32[]{:T(128)} %get-tuple-element.222, f32[]{:T(128)} %get-tuple-element.223), channel_id=1, replica_groups=mesh['groups'=2,'blk_0'=16,'blk_1'=4,'blk_2'=2] {'blk_2'}, use_global_device_ids=true, to_apply=%region_31.33 | all-reduce | flops 3 | bytes 24 | tf_op jit(solution)/shard_map/psum | solution.py:57
  (135 shorter events, 111.8 us)
Async XLA Ops:
  69.8 16.9 %collective-permute-start = (f32[6,32]{1,0:T(8,128)S(1)}, f32[6,32]{1,0:T(8,128)S(1)}, u32[]{:S(2)}, u32[]{:S(2)}) collective-permute-start(f32[6,32]{1,0:T(8,128)S(1)} %get-tuple-element.263), channel_id=1, source_target_pairs={{0,1},{1,2},{2,3},{3,4},{4,5},{5,6},{6,7},{7,8},{8,9},{9,10},{10,1... | collective-permute-start | bytes 2312 | tf_op jit(solution)/shard_map/ppermute | solution.py:25
  69.9 16.9 %collective-permute-start.1 = (f32[6,32]{1,0:T(8,128)S(1)}, f32[6,32]{1,0:T(8,128)S(1)}, u32[]{:S(2)}, u32[]{:S(2)}) collective-permute-start(f32[6,32]{1,0:T(8,128)S(1)} %get-tuple-element.264), channel_id=1, source_target_pairs={{1,0},{2,1},{3,2},{4,3},{5,4},{6,5},{7,6},{8,7},{9,8},{10,9},{11,1... | collective-permute-start | bytes 2312 | tf_op jit(solution)/shard_map/ppermute | solution.py:27
  71.7 7.5 %all-to-all-start = ((f32[4,1,6,256]{3,1,2,0:T(1,128)}), f32[4,1,6,256]{3,1,2,0:T(1,128)S(1)}, u32[]{:S(2)}, u32[]{:S(2)}) async-start(f32[4,1,6,256]{3,1,2,0:T(1,128)} %stack.66), calls=%async_computation | async-start | bytes 49152 | tf_op jit(solution)/shard_map/all_to_all | solution.py:45
  80.0 21.8 %all-to-all-start.1 = ((f32[16,4,6,256]{3,1,2,0:T(4,128)}), f32[16,4,6,256]{3,1,2,0:T(4,128)S(1)}, u32[]{:S(2)}, u32[]{:S(2)}) async-start(f32[16,4,6,256]{3,1,2,0:T(4,128)} %stack.67), calls=%async_computation.1 | async-start | bytes 786432 | tf_op jit(solution)/shard_map/all_to_all | solution.py:45
  99.2 1.7 copy-start.2
  114.6 0.7 copy-start
  115.3 66.1 %copy-start.1 = (f32[3,256]{1,0:T(4,128)S(1)}, f32[3,256]{1,0:T(4,128)}, u32[]{:S(2)}) copy-start(f32[3,256]{1,0:T(4,128)} %param.11) | copy-start | bytes 9220
  235.1 26.7 %all-to-all-start.4 = ((f32[16,4,6,256]{3,1,2,0:T(4,128)}), f32[16,4,6,256]{3,1,2,0:T(4,128)S(1)}, u32[]{:S(2)}, u32[]{:S(2)}) async-start(f32[16,4,6,256]{3,1,2,0:T(4,128)} %stack.70), calls=%async_computation.4 | async-start | bytes 786432 | tf_op jit(solution)/shard_map/all_to_all | solution.py:45
  242.5 3.1 collective-permute-start.2
  244.5 3.0 collective-permute-start.3
